TPU v7x, 128 devices: a whole 4x4x4 slice. The times are simulated.
128 devices in a mesh: dp: 1, tp: 2 (over core), ep: 64 (over z, y, x).
Axes of the slice: x: 4, y: 4, z: 4, core: 2. Of those that a mesh axis runs over, the one named last changes fastest.
Arguments:
- tokens_a: bfloat16 [16384, 2048], P(('dp', 'ep', 'tp'))
- expert_ids_a: int32 [16384, 6], P(('dp', 'ep', 'tp'))
- gates_a: float32 [16384, 6], P(('dp', 'ep', 'tp'))
- tokens_b: bfloat16 [16384, 2048], P(('dp', 'ep', 'tp'))
- expert_ids_b: int32 [16384, 6], P(('dp', 'ep', 'tp'))
- gates_b: float32 [16384, 6], P(('dp', 'ep', 'tp'))
- w_gate: bfloat16 [64, 2048, 1408], P('ep', None, 'tp')
- w_up: bfloat16 [64, 2048, 1408], P('ep', None, 'tp')
- w_down: bfloat16 [64, 1408, 2048], P('ep', 'tp')
Outputs:
- output 1: bfloat16 [16384, 2048], P(('dp', 'ep', 'tp'))
- output 2: bfloat16 [16384, 2048], P(('dp', 'ep', 'tp'))
All inputs are finite; a program needn't handle non-finite values.
Results may differ from a plain program's by a relative error of at most 0.00156.
Values are sent between devices in bfloat16 or wider.
A program may use at most 1 GiB of HBM per device.

v0:
```python
import jax
import jax.numpy as jnp
from jax import lax
from jax.sharding import PartitionSpec as P


def solution(mesh):
    ep_size = mesh.shape["ep"]
    row_spec = P(("dp", "ep", "tp"), None)
    gate_spec = P("ep", None, "tp")
    down_spec = P("ep", "tp", None)

    def moe_local(tokens, expert_ids, gate_vals, w_gate, w_up, w_down):
        tok_loc, model_dim = tokens.shape
        top_k = expert_ids.shape[1]
        num_experts = w_gate.shape[0] * ep_size
        mean_load = top_k * tok_loc // num_experts
        capacity = mean_load + mean_load // 4
        flat_ids = expert_ids.reshape(tok_loc * top_k)
        onehot = (flat_ids[:, None] == jnp.arange(num_experts, dtype=jnp.int32)[None, :]).astype(jnp.int32)
        position = jnp.sum(jnp.cumsum(onehot, axis=0) * onehot, axis=1) - 1
        slot_ids = jnp.where(position < capacity, flat_ids * capacity + position, num_experts * capacity)
        copy_tok = jnp.arange(tok_loc * top_k, dtype=jnp.int32) // top_k
        source = jnp.full((num_experts * capacity,), tok_loc, jnp.int32).at[slot_ids].set(copy_tok, mode="drop")
        slot_rows = jnp.take(tokens, source, axis=0, mode="fill", fill_value=0).reshape(num_experts, capacity, model_dim)
        received = lax.all_to_all(slot_rows, "ep", 0, 1, tiled=True)
        gathered = lax.all_gather(received, "tp", axis=1, tiled=True)
        gate_act = jnp.einsum("erd,edf->erf", gathered, w_gate, preferred_element_type=jnp.float32)
        up_lin = jnp.einsum("erd,edf->erf", gathered, w_up, preferred_element_type=jnp.float32)
        hidden = (jax.nn.silu(gate_act) * up_lin).astype(jnp.bfloat16)
        partial_out = jnp.einsum("erf,efd->erd", hidden, w_down, preferred_element_type=jnp.float32)
        summed = lax.psum_scatter(partial_out, "tp", scatter_dimension=1, tiled=True)
        returned = lax.all_to_all(summed.astype(jnp.bfloat16), "ep", 1, 0, tiled=True)
        copies = jnp.take(returned.reshape(num_experts * capacity, model_dim), slot_ids, axis=0, mode="fill", fill_value=0)
        weighted = copies.reshape(tok_loc, top_k, model_dim).astype(jnp.float32) * gate_vals[:, :, None]
        return jnp.sum(weighted, axis=1).astype(jnp.bfloat16)

    def group_body(tokens_a, expert_ids_a, gates_a, tokens_b, expert_ids_b, gates_b, w_gate, w_up, w_down):
        out_a = moe_local(tokens_a, expert_ids_a, gates_a, w_gate, w_up, w_down)
        out_b = moe_local(tokens_b, expert_ids_b, gates_b, w_gate, w_up, w_down)
        return (out_a, out_b)

    in_specs = (row_spec, row_spec, row_spec, row_spec, row_spec, row_spec, gate_spec, gate_spec, down_spec)
    return jax.shard_map(group_body, mesh=mesh, in_specs=in_specs, out_specs=(row_spec, row_spec), check_vma=False)
```

profile of v0, /device:TPU:3, one launch (start us, length us, event | category | flops | bytes accessed | tf_op | source)
XLA Modules:
  0.0 551.5 jit_solution(12826836262426527559)
XLA Ops:
  20.9 5.9 %gather_fusion = bf16[960,2048]{1,0:T(8,128)(2,1)} fusion(bf16[128,2048]{1,0:T(8,128)(2,1)S(1)} %copy-done.2, s32[1024]{0:T(1024)S(1)} %pad_clamp_fusion.3), kind=kCustom, calls=%fused_computation.clone | custom fusion | bytes 7868160 | tf_op jit(solution)/shard_map/jit(_take)/gather | solution.py:25
  31.1 5.1 reshape.207
  36.3 74.7 %all_to_all.42 = bf16[64,15,2048]{2,1,0:T(8,128)(2,1)} all-to-all(bf16[64,15,2048]{2,1,0:T(8,128)(2,1)} %reshape.207), channel_id=1, replica_groups=mesh['dp'=1,'tp'=2,'ep'=64] {'ep'}, dimensions={0} | all-to-all | bytes 7864320 | tf_op jit(solution)/shard_map/all_to_all | solution.py:26
  111.0 5.1 all_to_all.13
  128.3 6.0 %gather_fusion.2 = bf16[960,2048]{1,0:T(8,128)(2,1)} fusion(bf16[128,2048]{1,0:T(8,128)(2,1)S(1)} %copy-done.3, s32[1024]{0:T(1024)S(1)} %pad_clamp_fusion.1), kind=kCustom, calls=%fused_computation.2.clone | custom fusion | bytes 7868160 | tf_op jit(solution)/shard_map/jit(_take)/gather | solution.py:25
  138.6 5.1 reshape.214
  143.8 61.6 %all_to_all.43 = bf16[64,15,2048]{2,1,0:T(8,128)(2,1)} all-to-all(bf16[64,15,2048]{2,1,0:T(8,128)(2,1)} %reshape.214), channel_id=1, replica_groups=mesh['dp'=1,'tp'=2,'ep'=64] {'ep'}, dimensions={0} | all-to-all | bytes 7864320 | tf_op jit(solution)/shard_map/all_to_all | solution.py:26
  205.4 5.1 all_to_all.16
  211.2 11.6 %fusion.6 = f32[1920,704]{0,1:T(8,128)} fusion(bf16[1,1920,2048]{2,1,0:T(8,128)(2,1)} %all-gather.3.cloned.1.call-done, bf16[1,2048,704]{1,2,0:T(8,128)(2,1)} %param.19), kind=kOutput, calls=%fused_computation.16 | convolution fusion | flops 5536481280 | bytes 16154624 | tf_op jit(solution)/shard_map/erd,edf->erf/dot_general | solution.py:28
  222.8 20.1 %convolution_bitcast_fusion.1 = f32[1,1920,2048]{2,1,0:T(8,128)} fusion(bf16[1,704,2048]{2,1,0:T(8,128)(2,1)S(1)} %copy-done, f32[1920,704]{0,1:T(8,128)} %fusion.6, bf16[1,1920,2048]{2,1,0:T(8,128)(2,1)} %all-gather.3.cloned.1.call-done, bf16[1,2048,704]{1,2,0:T(8,128)(2,1)} %param.20), kind=kOutput, calls=%fused_computation.7 | convolution fusion | flops 11081072640 | bytes 34766848 | tf_op jit(solution)/shard_map/erf,efd->erd/dot_general | solution.py:31
  243.2 11.6 %fusion.2 = f32[1920,704]{0,1:T(8,128)} fusion(bf16[1,1920,2048]{2,1,0:T(8,128)(2,1)} %all-gather.5.cloned.1.call-done, bf16[1,2048,704]{1,2,0:T(8,128)(2,1)} %param.19), kind=kOutput, calls=%fused_computation.12 | convolution fusion | flops 5536481280 | bytes 16154624 | tf_op jit(solution)/shard_map/erd,edf->erf/dot_general | solution.py:28
  254.8 20.1 %convolution_bitcast_fusion = f32[1,1920,2048]{2,1,0:T(8,128)} fusion(bf16[1,704,2048]{2,1,0:T(8,128)(2,1)S(1)} %copy-done, f32[1920,704]{0,1:T(8,128)} %fusion.2, bf16[1,1920,2048]{2,1,0:T(8,128)(2,1)} %all-gather.5.cloned.1.call-done, bf16[1,2048,704]{1,2,0:T(8,128)(2,1)} %param.20), kind=kOutput, calls=%fused_computation.6 | convolution fusion | flops 11081072640 | bytes 34766848 | tf_op jit(solution)/shard_map/erf,efd->erd/dot_general | solution.py:31
  278.8 23.2 %copy.60 = bf16[1,960,2048]{2,0,1:T(2,128)(2,1)} copy(bf16[1,960,2048]{2,1,0:T(8,128)(2,1)S(1)} %convert_element_type.44) | data formatting | bytes 7864320 | tf_op jit(solution)/shard_map/convert_element_type | solution.py:33
  302.5 25.5 %reduce.9 = bf16[960,2048]{1,0:T(8,128)(2,1)} reduce(bf16[960,1,2048]{2,1,0:T(2,128)(2,1)} %bitcast.87, bf16[]{:T(256)} %broadcast.218), dimensions={1}, to_apply=%bitcast.82.reduce_sub_computation | reduce | bytes 7864322
  327.9 6.6 %reshape.287 = bf16[64,2,15360]{2,1,0:T(2,128)(2,1)} reshape(bf16[960,2048]{1,0:T(8,128)(2,1)} %reduce.9) | data formatting | bytes 7864320
  334.5 10.1 %all-to-all-start.1 = ((bf16[64,2,15360]{2,1,0:T(2,128)(2,1)}), bf16[64,2,15360]{2,1,0:T(2,128)(2,1)}, u32[]{:S(2)}, u32[]{:S(2)}) async-start(bf16[64,2,15360]{2,1,0:T(2,128)(2,1)} %reshape.287), calls=%async_computation.2 | async-start | bytes 7864320 | tf_op jit(solution)/shard_map/all_to_all | solution.py:33
  348.5 23.1 %copy.59 = bf16[1,960,2048]{2,0,1:T(2,128)(2,1)} copy(bf16[1,960,2048]{2,1,0:T(8,128)(2,1)S(1)} %convert_element_type.50) | data formatting | bytes 7864320 | tf_op jit(solution)/shard_map/convert_element_type | solution.py:33
  371.7 25.3 %reduce.8 = bf16[960,2048]{1,0:T(8,128)(2,1)} reduce(bf16[960,1,2048]{2,1,0:T(2,128)(2,1)} %bitcast.88, bf16[]{:T(256)} %broadcast.218), dimensions={1}, to_apply=%bitcast.81.reduce_sub_computation | reduce | bytes 7864322
  396.9 6.6 %reshape.289 = bf16[64,2,15360]{2,1,0:T(2,128)(2,1)} reshape(bf16[960,2048]{1,0:T(8,128)(2,1)} %reduce.8) | data formatting | bytes 7864320
  403.5 12.9 %all-to-all-start.3 = ((bf16[64,2,15360]{2,1,0:T(2,128)(2,1)}), bf16[64,2,15360]{2,1,0:T(2,128)(2,1)}, u32[]{:S(2)}, u32[]{:S(2)}) async-start(bf16[64,2,15360]{2,1,0:T(2,128)(2,1)} %reshape.289), calls=%async_computation.5 | async-start | bytes 7864320 | tf_op jit(solution)/shard_map/all_to_all | solution.py:33
  416.8 19.3 %reshape.288 = bf16[960,1,2048]{2,1,0:T(2,128)(2,1)} reshape(bf16[64,2,15360]{2,1,0:T(2,128)(2,1)} %all-to-all-done.1) | data formatting | bytes 7864320
  436.0 7.7 %copy.58 = bf16[1,960,2048]{2,1,0:T(8,128)(2,1)} copy(bf16[1,960,2048]{2,0,1:T(2,128)(2,1)} %bitcast.89) | data formatting | bytes 7864320
  443.7 9.7 %gather_fusion.1 = bf16[768,2048]{1,0:T(8,128)(2,1)} fusion(bf16[960,2048]{1,0:T(8,128)(2,1)} %bitcast.85, s32[1024]{0:T(1024)S(1)} %pad_clamp_fusion.2), kind=kCustom, calls=%fused_computation.1.clone | custom fusion | bytes 6294528 | tf_op jit(solution)/shard_map/jit(_take)/gather | solution.py:34
  453.5 5.1 select_convert_fusion.1
  458.5 7.8 %reshape.217 = f32[128,6,2048]{2,1,0:T(8,128)} reshape(f32[768,2048]{1,0:T(8,128)} %select_convert_fusion.1) | data formatting | bytes 12582912 | tf_op jit(solution)/shard_map/convert_element_type | solution.py:35
  466.4 17.7 %all-to-all-done.3 = bf16[64,2,15360]{2,1,0:T(2,128)(2,1)} async-done(((bf16[64,2,15360]{2,1,0:T(2,128)(2,1)}), bf16[64,2,15360]{2,1,0:T(2,128)(2,1)}, u32[]{:S(2)}, u32[]{:S(2)}) %all-to-all-start.3) | async-done | bytes 3932192 | tf_op jit(solution)/shard_map/all_to_all | solution.py:33
  484.0 19.3 %reshape.290 = bf16[960,1,2048]{2,1,0:T(2,128)(2,1)} reshape(bf16[64,2,15360]{2,1,0:T(2,128)(2,1)} %all-to-all-done.3) | data formatting | bytes 7864320
  503.3 7.6 %copy.57 = bf16[1,960,2048]{2,1,0:T(8,128)(2,1)} copy(bf16[1,960,2048]{2,0,1:T(2,128)(2,1)} %bitcast.90) | data formatting | bytes 7864320
  510.9 9.7 %gather_fusion.3 = bf16[768,2048]{1,0:T(8,128)(2,1)} fusion(bf16[960,2048]{1,0:T(8,128)(2,1)} %bitcast.86, s32[1024]{0:T(1024)S(1)} %pad_clamp_fusion), kind=kCustom, calls=%fused_computation.3.clone | custom fusion | bytes 6294528 | tf_op jit(solution)/shard_map/jit(_take)/gather | solution.py:34
  520.6 5.0 select_convert_fusion
  525.6 8.0 %reshape.218 = f32[128,6,2048]{2,1,0:T(8,128)} reshape(f32[768,2048]{1,0:T(8,128)} %select_convert_fusion) | data formatting | bytes 12582912 | tf_op jit(solution)/shard_map/convert_element_type | solution.py:35
  533.6 11.2 %multiply_reduce_fusion = (bf16[128,2048]{1,0:T(8,128)(2,1)}, bf16[128,2048]{1,0:T(8,128)(2,1)}) fusion(f32[128,6,2048]{2,1,0:T(8,128)} %reshape.218, f32[128,6]{1,0:T(8,128)S(1)} %copy.46, f32[128,6,2048]{2,1,0:T(8,128)} %reshape.217, f32[128,6]{1,0:T(8,128)S(1)} %copy.40), kind=kLoop, calls=%fused_computation.8 | loop fusion | flops 5767168 | bytes 13637632 | tf_op jit(solution)/shard_map/reduce_sum | solution.py:36
  (81 shorter events, 43.8 us)
Async XLA Ops:
  7.2 215.6 %copy-start = (bf16[1,704,2048]{2,1,0:T(8,128)(2,1)S(1)}, bf16[1,704,2048]{2,1,0:T(8,128)(2,1)}, u32[]{:S(2)}) copy-start(bf16[1,704,2048]{2,1,0:T(8,128)(2,1)} %param.21) | copy-start | bytes 8650756
  7.2 13.7 %copy-start.2 = (bf16[128,2048]{1,0:T(8,128)(2,1)S(1)}, bf16[128,2048]{1,0:T(8,128)(2,1)}, u32[]{:S(2)}) copy-start(bf16[128,2048]{1,0:T(8,128)(2,1)} %param.13) | copy-start | bytes 1572868
  7.2 204.0 %all-gather.3.cloned.1.call-start = ((), (), s32[]{:S(2)}) async-start(), calls=%async_computation.6 | async-start | bytes 11796480 | tf_op jit(solution)/shard_map/all_gather | solution.py:27
  8.5 18.3 %copy-start.4 = (s32[768]{0:T(1024)}, s32[768]{0:T(1024)S(1)}, u32[]{:S(2)}) copy-start(s32[768]{0:T(1024)S(1)} %eq.50) | copy-start | bytes 9220
  16.6 0.6 copy-start.6
  116.1 0.7 copy-start.8
  116.1 12.2 %copy-start.3 = (bf16[128,2048]{1,0:T(8,128)(2,1)S(1)}, bf16[128,2048]{1,0:T(8,128)(2,1)}, u32[]{:S(2)}) copy-start(bf16[128,2048]{1,0:T(8,128)(2,1)} %param.16) | copy-start | bytes 1572868
  116.1 127.1 %all-gather.5.cloned.1.call-start = ((), (), s32[]{:S(2)}) async-start(), calls=%async_computation.8 | async-start | bytes 11796480 | tf_op jit(solution)/shard_map/all_gather | solution.py:27
  210.6 64.4 %reduce-scatter.3.cloned.1.call-start = ((), (), s32[]{:S(2)}) async-start(), calls=%async_computation.7 | async-start | bytes 23592960 | tf_op jit(solution)/shard_map/reduce_scatter | solution.py:32
  243.0 101.7 %reduce-scatter.5.cloned.1.call-start = ((), (), s32[]{:S(2)}) async-start(), calls=%async_computation.9 | async-start | bytes 23592960 | tf_op jit(solution)/shard_map/reduce_scatter | solution.py:32
  334.5 69.0 %all-to-all-start.1 = ((bf16[64,2,15360]{2,1,0:T(2,128)(2,1)}), bf16[64,2,15360]{2,1,0:T(2,128)(2,1)}, u32[]{:S(2)}, u32[]{:S(2)}) async-start(bf16[64,2,15360]{2,1,0:T(2,128)(2,1)} %reshape.287), calls=%async_computation.2 | async-start | bytes 7864320 | tf_op jit(solution)/shard_map/all_to_all | solution.py:33
  403.5 12.9 %copy-start.9 = (f32[128,6]{0,1:T(8,128)S(1)}, f32[128,6]{0,1:T(8,128)}, u32[]{:S(2)}) copy-start(f32[128,6]{0,1:T(8,128)} %param.15) | copy-start | bytes 9220
  403.5 13.1 %copy-start.10 = (f32[128,6]{0,1:T(8,128)S(1)}, f32[128,6]{0,1:T(8,128)}, u32[]{:S(2)}) copy-start(f32[128,6]{0,1:T(8,128)} %param.18) | copy-start | bytes 9220
  403.5 13.2 %copy-start.5 = (s32[768]{0:T(1024)S(1)}, s32[768]{0:T(1024)}, u32[]{:S(2)}) copy-start(s32[768]{0:T(1024)} %copy-done.4) | copy-start | bytes 9220
  403.5 13.2 %copy-start.7 = (s32[768]{0:T(1024)S(1)}, s32[768]{0:T(1024)}, u32[]{:S(2)}) copy-start(s32[768]{0:T(1024)} %copy-done.6) | copy-start | bytes 9220
  403.5 80.5 %all-to-all-start.3 = ((bf16[64,2,15360]{2,1,0:T(2,128)(2,1)}), bf16[64,2,15360]{2,1,0:T(2,128)(2,1)}, u32[]{:S(2)}, u32[]{:S(2)}) async-start(bf16[64,2,15360]{2,1,0:T(2,128)(2,1)} %reshape.289), calls=%async_computation.5 | async-start | bytes 7864320 | tf_op jit(solution)/shard_map/all_to_all | solution.py:33
  533.6 11.2 %copy-start.1 = (bf16[1,704,2048]{2,1,0:T(8,128)(2,1)S(1)}, bf16[1,704,2048]{2,1,0:T(8,128)(2,1)}, u32[]{:S(2)}) copy-start(bf16[1,704,2048]{2,1,0:T(8,128)(2,1)} %param.21) | copy-start | bytes 8650756
Sparse Core Ops, SparseCore 0:
  116.2 17.5 all-gather.2
  210.7 24.2 all-gather.4
  243.1 24.8 reduce-scatter.2
  275.1 24.8 reduce-scatter.4
where the time goes:
time: 562 us; the launch traced here: 552 us
  local copies, waits for them, and re-layouts  194 us (35%)
  blocking collectives  136 us (24%)
  other arithmetic  102 us (18%)
  matrix products  63.5 us (11%)
  starting transfers between devices  23.9 us (4%)
  waiting for transfers between devices  17.8 us (3%)
  between operations  14.3 us (3%)
    all_to_all x2, blocking collectives, moe_local(): received = lax.all_to_all(slot_rows, 'ep', 0, 1, tiled=True)  136 us
    unnamed x33, local copies, waits for them, and re-layouts  70 us
    unnamed x2, other arithmetic  50.7 us
    convert_element_type x2, local copies, waits for them, and re-layouts, moe_local(): summed.astype(jnp.bfloat16)  46.3 us
    dot_general x2, matrix products, moe_local(): jnp.einsum('erf,efd->erd', hidden, w_down, preferred_element_type=jnp.flo...  40.3 us
    dot_general x2, matrix products, moe_local(): jnp.einsum('erd,edf->erf', gathered, w_gate, preferred_element_type=jnp.f...  23.2 us
    all_to_all x2, starting transfers between devices, moe_local(): lax.all_to_all(summed.astype(jnp.bfloat16), 'ep', 1, 0, tiled=True)  23.1 us
    gather x2, local copies, waits for them, and re-layouts, moe_local(): jnp.take(returned.reshape(num_experts * capacity, model_dim), slot_ids, a...  19.4 us
  transfers between devices with their start and end apart: 6, of which 1 were waited for; matrix products, arithmetic and copies ran while one was open for 47% of the time, Pallas kernels for 0%

commit v1 on v0

v1 whole, which is shorter than its diff:
```python
import jax
import jax.numpy as jnp
from jax import lax
from jax.experimental import pallas as pl
from jax.experimental.pallas import tpu as pltpu
from jax.sharding import PartitionSpec as P

MESH_ID = pl.DeviceIdType.MESH
SLOT = 16
CAP = 15
TOK = 128
DIM = 2048
STRIDE = (16, 4, 1)
CHUNKS = ((0, 0, 384), (1, 384, 384), (2, 768, 384), (0, 1152, 384), (1, 1536, 256), (2, 1792, 256))
NCH = len(CHUNKS)


def moe_kernel(tok_a, tok_b, idt, ids_a, ids_b, gate_a, gate_b, wg_in, wu_in, wd_in,
               out_a, out_b, relay_in, relay_out,
               idbuf, gath, send2, rows, turn, fin, wg, wu, wd, sel, comb,
               id_s, id_r, w_s, w_r, w_l, own1,
               d1s, d1r, d2s, d2r, d3s, d3r, r1s, r1r, r2s, r2r, r3s, r3r, own2, own3, own5, own6):
    f32, bf16 = jnp.float32, jnp.bfloat16
    ep = lax.axis_index("ep")
    tp = lax.axis_index("tp")
    me = (ep // 16, lax.rem(ep // 4, 4), lax.rem(ep, 4))
    toks, outs = (tok_a, tok_b), (out_a, out_b)
    ids_n, gates_n = (ids_a, ids_b), (gate_a, gate_b)

    def shifted(axis, step):
        return lax.rem(me[axis] + step, 4)

    def peer(axis, step):
        return {"ep": ep + (shifted(axis, step) - me[axis]) * STRIDE[axis]}

    def remote(src, dst, s_sem, r_sem, dev):
        return pltpu.make_async_remote_copy(src, dst, s_sem, r_sem, device_id=dev, device_id_type=MESH_ID)

    def cols(k):
        return pl.ds(CHUNKS[k][1], CHUNKS[k][2])

    def fixed_canon(buf, bt, axis, at, k):
        if axis == 0:
            return buf.at[bt, at, :, :, :, cols(k)]
        if axis == 1:
            return buf.at[bt, :, at, :, :, cols(k)]
        return buf.at[bt, :, :, at, :, cols(k)]

    def relay_slot(buf, bt, o, k, at):
        if o == 2:
            return buf.at[bt, :, at, :, :, cols(k)]
        return buf.at[bt, :, :, at, :, cols(k)]

    def copy_d1(bt, k, i):
        o = CHUNKS[k][0]
        return remote(toks[bt].at[:, cols(k)], gath.at[bt, me[o], :, cols(k)],
                      d1s.at[bt, k, i - 1], d1r.at[bt, k, i - 1], peer(o, i))

    def local_d1(bt, k):
        o = CHUNKS[k][0]
        return pltpu.make_async_copy(toks[bt].at[:, cols(k)], gath.at[bt, me[o], :, cols(k)], own1.at[bt, k])

    def copy_d2(bt, k, i):
        o = CHUNKS[k][0]
        b = (o + 1) % 3
        return remote(send2.at[shifted(b, i), :, :, :, cols(k)], relay_slot(relay_in, bt, o, k, me[b]),
                      d2s.at[bt, k, i - 1], d2r.at[bt, k, i - 1], peer(b, i))

    def local_d2(bt, k):
        o = CHUNKS[k][0]
        b = (o + 1) % 3
        return pltpu.make_async_copy(send2.at[me[b], :, :, :, cols(k)], relay_slot(relay_in, bt, o, k, me[b]), own2.at[bt, k])

    def copy_3(src, dst, s, r, bt, k, i):
        c = (CHUNKS[k][0] + 2) % 3
        return remote(src.at[bt, shifted(c, i), :, :, :, cols(k)], fixed_canon(dst, bt, c, me[c], k),
                      s.at[bt, k, i - 1], r.at[bt, k, i - 1], peer(c, i))

    def local_3(src, dst, sem, bt, k):
        c = (CHUNKS[k][0] + 2) % 3
        return pltpu.make_async_copy(src.at[bt, me[c], :, :, :, cols(k)], fixed_canon(dst, bt, c, me[c], k), sem.at[bt, k])

    def copy_r1(bt, k, i):
        o = CHUNKS[k][0]
        return remote(fixed_canon(rows, bt, o, shifted(o, i), k), turn.at[bt, :, :, me[o], :, cols(k)],
                      r1s.at[bt, k, i - 1], r1r.at[bt, k, i - 1], peer(o, i))

    def turn_part(bt, k, at):
        if CHUNKS[k][0] == 1:
            return turn.at[bt, :, at, :, :, cols(k)]
        return turn.at[bt, at, :, :, :, cols(k)]

    def copy_r2(bt, k, i):
        o = CHUNKS[k][0]
        b = (o + 1) % 3
        return remote(turn_part(bt, k, shifted(b, i)), relay_slot(relay_out, bt, o, k, me[b]),
                      r2s.at[bt, k, i - 1], r2r.at[bt, k, i - 1], peer(b, i))

    def local_r2(bt, k):
        o = CHUNKS[k][0]
        b = (o + 1) % 3
        return pltpu.make_async_copy(turn_part(bt, k, me[b]), relay_slot(relay_out, bt, o, k, me[b]), own5.at[bt, k])

    def copy_d3(bt, k, i):
        return copy_3(relay_in, rows, d3s, d3r, bt, k, i)

    def copy_r3(bt, k, i):
        return copy_3(relay_out, fin, r3s, r3r, bt, k, i)

    def local_d3(bt, k):
        return local_3(relay_in, rows, own3, bt, k)

    def local_r3(bt, k):
        return local_3(relay_out, fin, own6, bt, k)

    def start3(copy, bt, k):
        for i in (2, 1, 3):
            copy(bt, k, i).start()

    def recv3(copy, bt, k):
        for i in (1, 3, 2):
            copy(bt, k, i).wait_recv()

    def sent3(copy, bt, k):
        for i in (1, 2, 3):
            copy(bt, k, i).wait_send()

    barrier = pltpu.get_barrier_semaphore()
    for axis in range(3):
        for i in (1, 2, 3):
            pl.semaphore_signal(barrier, inc=1, device_id=peer(axis, i), device_id_type=MESH_ID)
    other = {"tp": 1 - tp}
    pl.semaphore_signal(barrier, inc=1, device_id=other, device_id_type=MESH_ID)
    for bt in (0, 1):
        for k in range(NCH):
            local_d1(bt, k).start()
    weights = ((wg_in, wg), (wu_in, wu), (wd_in, wd))

    def weight_local(n):
        src, dst = weights[n]
        return pltpu.make_async_copy(src.at[0], dst.at[tp], w_l.at[n])

    def weight_remote(n):
        src, dst = weights[n]
        return remote(src.at[0], dst.at[tp], w_s.at[n], w_r.at[n], other)

    def id_copy(axis, i):
        return remote(idt, idbuf.at[axis, me[axis]], id_s.at[axis, i - 1], id_r.at[axis, i - 1], peer(axis, i))

    for n in range(3):
        weight_local(n).start()
    for axis in range(3):
        idbuf[axis, me[axis]] = idt[...]

    pl.semaphore_wait(barrier, 10)
    for axis in range(3):
        for i in (2, 1, 3):
            id_copy(axis, i).start()
    for k in range(NCH):
        start3(copy_d1, 0, k)
    for n in range(3):
        weight_remote(n).start()

    def iota(shape, dim):
        return lax.broadcasted_iota(jnp.int32, shape, dim)

    def build_comb(bt):
        ids, gates = ids_n[bt][...], gates_n[bt][...]
        expert = iota((TOK, 64), 1)
        hit = jnp.zeros((TOK, 64), f32)
        gate = jnp.zeros((TOK, 64), f32)
        for j in range(ids.shape[1]):
            same = ids[:, j:j + 1] == expert
            hit = jnp.where(same, 1.0, hit)
            gate = jnp.where(same, gates[:, j:j + 1], gate)
        before = jnp.where(iota((TOK, TOK), 1) < iota((TOK, TOK), 0), 1.0, 0.0).astype(bf16)
        count = jnp.dot(before, hit.astype(bf16), preferred_element_type=f32)
        place = jnp.where((hit > 0.5) & (count < CAP - 0.5), count, -1.0)
        spread = jnp.where(iota((64, 64 * SLOT), 1) // SLOT == iota((64, 64 * SLOT), 0), 1.0, 0.0).astype(bf16)
        wide = jnp.dot(place.astype(bf16), spread, preferred_element_type=f32)
        at_slot = wide == lax.rem(iota((TOK, 64 * SLOT), 1), SLOT).astype(f32)
        rest = gate
        for n in range(3):
            part = rest.astype(bf16)
            rest = rest - part.astype(f32)
            part_wide = jnp.dot(part, spread, preferred_element_type=f32)
            comb[bt, n * TOK:(n + 1) * TOK, :] = jnp.where(at_slot, part_wide, 0.0).astype(bf16)

    def build_sel(bt):
        before = jnp.where(iota((TOK, TOK), 0) < iota((TOK, TOK), 1), 1.0, 0.0).astype(bf16)
        for o in range(3):
            b, c = (o + 1) % 3, (o + 2) % 3
            row = iota((16, TOK), 0)
            expert = me[o] * STRIDE[o] + (row // 4) * STRIDE[b] + lax.rem(row, 4) * STRIDE[c]
            for a in range(4):
                ids = idbuf[o, a, bt * 8:bt * 8 + 8, :]
                hit = jnp.zeros((16, TOK), f32)
                for j in range(6):
                    hit = jnp.where(ids[j:j + 1, :] == expert, 1.0, hit)
                count = jnp.dot(hit.astype(bf16), before, preferred_element_type=f32)
                place = jnp.where((hit > 0.5) & (count < CAP - 0.5), count, -1.0)
                slot = iota((SLOT, TOK), 0).astype(f32)
                for r in range(16):
                    sel[bt, o, a, r * SLOT:(r + 1) * SLOT, :] = jnp.where(place[r:r + 1, :] == slot, 1.0, 0.0).astype(bf16)

    def step_d2(bt, k):
        o, c0, w = CHUNKS[k]
        local_d1(bt, k).wait()
        recv3(copy_d1, bt, k)
        if bt == 1:
            sent3(copy_d2, 0, k)
        for a in range(4):
            got = jnp.dot(sel[bt, o, a], gath[bt, a, :, c0:c0 + w], preferred_element_type=f32)
            send2[:, :, a, :, c0:c0 + w] = got.astype(bf16).reshape(4, 4, SLOT, w)
        start3(copy_d2, bt, k)
        local_d2(bt, k).start()

    def step_d3(bt, k):
        local_d2(bt, k).wait()
        recv3(copy_d2, bt, k)
        start3(copy_d3, bt, k)
        local_d3(bt, k).start()

    def wait_rows(bt):
        for k in range(NCH):
            recv3(copy_d3, bt, k)
            local_d3(bt, k).wait()

    def ffn(bt, m):
        x = rows[bt, m].reshape(256, DIM)
        total = None
        for h in (0, 1):
            g = jnp.dot(x, wg[h], preferred_element_type=f32)
            u = jnp.dot(x, wu[h], preferred_element_type=f32)
            hid = (jax.nn.silu(g) * u).astype(bf16)
            part = jnp.dot(hid, wd[h], preferred_element_type=f32)
            total = part if total is None else total + part
        rows[bt, m] = total.astype(bf16).reshape(4, 4, SLOT, DIM)

    def step_r1(bt):
        for k in range(NCH):
            start3(copy_r1, bt, k)
        for k in range(NCH):
            o, c0, w = CHUNKS[k]
            cs = slice(c0, c0 + w)
            if o == 0:
                turn[bt, :, :, me[0], :, cs] = rows[bt, me[0], :, :, :, cs]
            elif o == 1:
                turn[bt, :, :, me[1], :, cs] = rows[bt, :, me[1], :, :, cs]
            else:
                turn[bt, :, :, me[2], :, cs] = rows[bt, :, :, me[2], :, cs]

    def step_r2(bt, k):
        recv3(copy_r1, bt, k)
        start3(copy_r2, bt, k)
        local_r2(bt, k).start()

    def step_r3(bt, k):
        recv3(copy_r2, bt, k)
        local_r2(bt, k).wait()
        start3(copy_r3, bt, k)
        local_r3(bt, k).start()

    def step_out(bt, k):
        o, c0, w = CHUNKS[k]
        recv3(copy_r3, bt, k)
        local_r3(bt, k).wait()
        vals = fin[bt, :, :, :, :, c0:c0 + w].reshape(64 * SLOT, w)
        got = jnp.dot(comb[bt], vals, preferred_element_type=f32)
        outs[bt][:, c0:c0 + w] = (got[:TOK] + got[TOK:2 * TOK] + got[2 * TOK:]).astype(bf16)

    for axis in range(3):
        for i in (1, 3, 2):
            id_copy(axis, i).wait_recv()
    build_sel(0)
    step_d2(0, 0)
    step_d2(0, 1)
    step_d2(0, 2)
    for k in range(NCH):
        start3(copy_d1, 1, k)
    for k in range(3):
        step_d2(0, k + 3)
        step_d3(0, k)
    build_sel(1)
    for k in range(3):
        step_d3(0, k + 3)
        step_d2(1, k)
    for n in range(3):
        weight_local(n).wait()
        weight_remote(n).wait_recv()
    wait_rows(0)

    after = {
        0: [lambda: step_d2(1, 3), lambda: step_d2(1, 4), lambda: step_d2(1, 5), lambda: step_d3(1, 0)],
        1: [lambda: step_d3(1, 1), lambda: step_d3(1, 2), lambda: step_d3(1, 3)],
        2: [lambda: step_d3(1, 4), lambda: step_d3(1, 5), lambda: build_comb(0), lambda: build_comb(1)],
        3: [lambda: step_r1(0), lambda: wait_rows(1)],
        4: [lambda: step_r2(0, 0), lambda: step_r2(0, 1), lambda: step_r2(0, 2)],
        5: [lambda: step_r2(0, 3), lambda: step_r2(0, 4), lambda: step_r2(0, 5), lambda: step_r3(0, 0)],
        6: [lambda: step_r3(0, 1), lambda: step_r3(0, 2), lambda: step_r3(0, 3)],
        7: [lambda: step_r1(1), lambda: step_r3(0, 4), lambda: step_r3(0, 5)],
    }

    def loop(step, carry):
        ffn(step // 4, lax.rem(step, 4))
        for at, todo in after.items():
            @pl.when(step == at)
            def _():
                for one in todo:
                    one()
        return carry

    lax.fori_loop(0, 8, loop, 0)

    for k in range(NCH):
        step_r2(1, k)
        step_out(0, k)
        if k >= 1:
            step_r3(1, k - 1)
    step_r3(1, NCH - 1)
    for k in range(NCH):
        step_out(1, k)

    for axis in range(3):
        for i in (1, 2, 3):
            id_copy(axis, i).wait_send()
    for n in range(3):
        weight_remote(n).wait_send()
    for bt in (0, 1):
        for k in range(NCH):
            sent3(copy_d1, bt, k)
            if bt == 1:
                sent3(copy_d2, bt, k)
            sent3(copy_d3, bt, k)
            sent3(copy_r1, bt, k)
            sent3(copy_r2, bt, k)
            sent3(copy_r3, bt, k)


def solution(mesh):
    row_spec = P(("dp", "ep", "tp"), None)
    gate_spec = P("ep", None, "tp")
    down_spec = P("ep", "tp", None)
    bf16 = jnp.bfloat16
    dma = pltpu.SemaphoreType.DMA

    def body(tok_a, ids_a, gate_a, tok_b, ids_b, gate_b, wg, wu, wd):
        pad = ((0, 2), (0, 0))
        idt = jnp.concatenate([jnp.pad(ids_a.T, pad, constant_values=-1), jnp.pad(ids_b.T, pad, constant_values=-1)])
        vmem = pl.BlockSpec(memory_space=pltpu.VMEM)
        hbm = pl.BlockSpec(memory_space=pl.ANY)
        half = wg.shape[2]
        box = (2, 4, 4, 4, SLOT, DIM)
        out = jax.ShapeDtypeStruct((TOK, DIM), bf16)
        relay = jax.ShapeDtypeStruct(box, bf16)
        stage = [dma((2, NCH, 3))] * 12
        res = pl.pallas_call(
            moe_kernel,
            out_shape=(out, out, relay, relay),
            in_specs=[hbm, hbm, vmem, vmem, vmem, vmem, vmem, hbm, hbm, hbm],
            out_specs=(vmem, vmem, hbm, hbm),
            scratch_shapes=[
                pltpu.VMEM((3, 4, 16, TOK), jnp.int32),
                pltpu.VMEM((2, 4, TOK, DIM), bf16),
                pltpu.VMEM((4, 4, 4, SLOT, DIM), bf16),
                pltpu.VMEM(box, bf16),
                pltpu.VMEM(box, bf16),
                pltpu.VMEM(box, bf16),
                pltpu.VMEM((2, DIM, half), bf16),
                pltpu.VMEM((2, DIM, half), bf16),
                pltpu.VMEM((2, half, DIM), bf16),
                pltpu.VMEM((2, 3, 4, 256, TOK), bf16),
                pltpu.VMEM((2, 3 * TOK, 64 * SLOT), bf16),
                dma((3, 3)), dma((3, 3)), dma((3,)), dma((3,)), dma((3,)), dma((2, NCH)),
                *stage,
                dma((2, NCH)), dma((2, NCH)), dma((2, NCH)), dma((2, NCH)),
            ],
            compiler_params=pltpu.CompilerParams(collective_id=0, has_side_effects=True, vmem_limit_bytes=67043328),
            name="moe",
        )(tok_a, tok_b, idt, ids_a, ids_b, gate_a, gate_b, wg, wu, wd)
        return res[0], res[1]

    specs = (row_spec,) * 6 + (gate_spec, gate_spec, down_spec)
    return jax.shard_map(body, mesh=mesh, in_specs=specs, out_specs=(row_spec, row_spec), check_vma=False)
```

time: 562 us -> 219 us (0.39); the launches traced: 552 us -> 218 us
  Pallas kernels: 0 us -> 199 us
  local copies, waits for them, and re-layouts: 194 us -> 17 us
  blocking collectives: 136 us -> 0 us
  other arithmetic: 102 us -> 1.31 us
  matrix products: 63.5 us -> 0 us
  starting transfers between devices: 23.9 us -> 0 us
  waiting for transfers between devices: 17.8 us -> 0 us
  between operations: 14.3 us -> 0.64 us
    pallas_call x0 -> x1, Pallas kernels: none -> 199 us  [body(): pl.pallas_call(moe_kernel, out_shape=(out, out, relay, relay), in_specs=[...]
    all_to_all x2 -> x0, blocking collectives: 136 us -> none  [moe_local(): received = lax.all_to_all(slot_rows, 'ep', 0, 1, tiled=True)]
    dot_general x4 -> x0, matrix products: 63.5 us -> none  [the longest x2 40.3 us: moe_local(): jnp.einsum('erf,efd->erd', hidden, w_down, preferred_element_type=jnp.flo...]
    convert_element_type x4 -> x0, local copies, waits for them, and re-layouts: 62.1 us -> none  [the longest x2 46.3 us: moe_local(): summed.astype(jnp.bfloat16)]
    unnamed x33 -> x10, local copies, waits for them, and re-layouts: 70 us -> 17 us
    unnamed x2 -> x0, other arithmetic: 50.7 us -> none
    gather x4 -> x0, local copies, waits for them, and re-layouts: 31.3 us -> none  [the longest x2 19.4 us: moe_local(): jnp.take(returned.reshape(num_experts * capacity, model_dim), slot_ids, a...]
    all_to_all x2 -> x0, starting transfers between devices: 23.1 us -> none  [moe_local(): lax.all_to_all(summed.astype(jnp.bfloat16), 'ep', 1, 0, tiled=True)]
  transfers between devices with their start and end apart: 6 -> 0, of which waited for: 1 -> 0; matrix products, arithmetic and copies ran while one was open for 47% -> 0% of each run, Pallas kernels for 0% -> 0%
where the time goes in v1:
time: 219 us; the launch traced here: 218 us
  Pallas kernels  199 us (91%)
  local copies, waits for them, and re-layouts  17 us (8%)
    pallas_call x1, Pallas kernels, body(): pl.pallas_call(moe_kernel, out_shape=(out, out, relay, relay), in_specs=[...  199 us
    unnamed x10, local copies, waits for them, and re-layouts  17 us

profile of v1, /device:TPU:3, one launch (start us, length us, event | category | flops | bytes accessed | tf_op | source)
XLA Modules:
  0.0 217.7 jit_solution(1115626366357879971)
XLA Ops:
  0.6 1.3 select_add_fusion.idt
  1.9 0.0 copy-start
  1.9 1.6 copy.13.gate_a
  3.5 1.4 copy.14.gate_b
  4.9 1.4 copy.11.ids_a
  6.3 1.4 copy.12.ids_b
  7.8 4.6 %copy.15.wg_in = bf16[1,2048,704]{2,1,0:T(8,128)(2,1)} copy(bf16[1,2048,704]{1,2,0:T(8,128)(2,1)} %param.15) | data formatting | bytes 5767168 | tf_op args[6]
  12.4 0.0 copy-done
  12.4 2.8 %copy.16.wu_in = bf16[1,2048,704]{2,1,0:T(8,128)(2,1)} copy(bf16[1,2048,704]{1,2,0:T(8,128)(2,1)S(1)} %copy-done) | data formatting | bytes 5767168 | tf_op args[7]
  15.2 198.8 %moe.1 = (bf16[128,2048]{1,0:T(8,128)(2,1)}, bf16[128,2048]{1,0:T(8,128)(2,1)}, bf16[2,4,4,4,16,2048]{5,4,3,2,1,0:T(8,128)(2,1)}, bf16[2,4,4,4,16,2048]{5,4,3,2,1,0:T(8,128)(2,1)}) custom-call(bf16[128,2048]{1,0:T(8,128)(2,1)} %tok_a.1, bf16[128,2048]{1,0:T(8,128)(2,1)} %tok_b.1, s32[16,128]{1,0:T(8,128)} %select_add_fusion.idt, s32[128,6]{1,0:T(8,128)} %copy.11.ids_a, ...), custom_call_target="tpu_custom_call" | custom-call | tf_op jit(solution)/shard_map/moe/pallas_call | solution.py:357
  213.9 1.9 copy.19
  215.8 1.9 copy.20
Async XLA Ops:
  1.9 10.4 %copy-start = (bf16[1,2048,704]{1,2,0:T(8,128)(2,1)S(1)}, bf16[1,2048,704]{1,2,0:T(8,128)(2,1)}, u32[]{:S(2)}) copy-start(bf16[1,2048,704]{1,2,0:T(8,128)(2,1)} %param.16) | copy-start | bytes 8650756

commit v2 on v1

--- a/solution.py
+++ b/solution.py
@@ -13,18 +13,45 @@
 STRIDE = (16, 4, 1)
 CHUNKS = ((0, 0, 384), (1, 384, 384), (2, 768, 384), (0, 1152, 384), (1, 1536, 256), (2, 1792, 256))
 NCH = len(CHUNKS)
-
-
-def moe_kernel(tok_a, tok_b, idt, ids_a, ids_b, gate_a, gate_b, wg_in, wu_in, wd_in,
-               out_a, out_b, relay_in, relay_out,
-               idbuf, gath, send2, rows, turn, fin, wg, wu, wd, sel, comb,
+BEFORE = (
+    ("D1", 0, 4), ("D1", 0, 2), ("D1", 0, 1), ("D1", 0, 3), ("D1", 0, 5), ("D1", 0, 0),
+    ("S", 0, 0), ("D1", 1, 2), ("D1", 1, 4), ("D1", 1, 3), ("D1", 1, 1), ("D1", 1, 5),
+    ("D2", 0, 4), ("D2", 0, 2), ("D2", 0, 5), ("D2", 0, 0), ("D2", 0, 1), ("S", 1, 0),
+    ("D2", 0, 3), ("D3", 0, 4), ("D1", 1, 0), ("D3", 0, 0), ("D3", 0, 2), ("D3", 0, 3),
+    ("D3", 0, 1), ("D2", 1, 4), ("D2", 1, 2), ("D3", 0, 5), ("W", 0, 0), ("D2", 1, 0),
+    ("D2", 1, 3), ("D2", 1, 1),
+)
+WHILE = {
+    2: (("D2", 1, 5), ("D3", 1, 0), ("D3", 1, 2), ("D3", 1, 4),),
+    7: (("D3", 1, 1), ("D3", 1, 3), ("D3", 1, 5),),
+    11: (("R1", 0, 2), ("R1", 0, 0), ("R1", 0, 4), ("R1", 0, 1),),
+    13: (("R1", 0, 3), ("R1", 0, 5), ("R2", 0, 4),),
+    14: (("R2", 0, 0),),
+    15: (("R2", 0, 2),),
+    19: (("R2", 0, 3), ("R2", 0, 1),),
+    21: (("R2", 0, 5),),
+    22: (("R3", 0, 2), ("R3", 0, 4), ("R3", 0, 0),),
+}
+AFTER = (
+    ("R1", 1, 3), ("R1", 1, 1), ("R1", 1, 2), ("R1", 1, 0), ("R3", 0, 1), ("W", 1, 0),
+    ("R3", 0, 3), ("R1", 1, 5), ("C", 0, 4), ("R1", 1, 4), ("R2", 1, 2), ("R2", 1, 3),
+    ("R2", 1, 0), ("C", 0, 3), ("R2", 1, 1), ("R2", 1, 4), ("R3", 0, 5), ("R3", 1, 3),
+    ("R2", 1, 5), ("R3", 1, 2), ("R3", 1, 1), ("C", 0, 1), ("R3", 1, 4), ("R3", 1, 5),
+    ("R3", 1, 0), ("C", 0, 0), ("C", 0, 5), ("C", 1, 3), ("C", 0, 2), ("C", 1, 1),
+    ("C", 1, 2), ("C", 1, 4), ("C", 1, 5), ("C", 1, 0),
+)
+
+
+def moe_kernel(tok_a, tok_b, ids_a, ids_b, gate_a, gate_b, wg_in, wu_in, wd_in,
+               out, relay_in, relay_out,
+               idbuf, gath, send2, rows, turn, fin, wg, wu, wd, hid, sel, comb,
                id_s, id_r, w_s, w_r, w_l, own1,
                d1s, d1r, d2s, d2r, d3s, d3r, r1s, r1r, r2s, r2r, r3s, r3r, own2, own3, own5, own6):
     f32, bf16 = jnp.float32, jnp.bfloat16
     ep = lax.axis_index("ep")
     tp = lax.axis_index("tp")
     me = (ep // 16, lax.rem(ep // 4, 4), lax.rem(ep, 4))
-    toks, outs = (tok_a, tok_b), (out_a, out_b)
+    toks = (tok_a, tok_b)
     ids_n, gates_n = (ids_a, ids_b), (gate_a, gate_b)
 
     def shifted(axis, step):
@@ -145,37 +172,36 @@
         return remote(src.at[0], dst.at[tp], w_s.at[n], w_r.at[n], other)
 
     def id_copy(axis, i):
-        return remote(idt, idbuf.at[axis, me[axis]], id_s.at[axis, i - 1], id_r.at[axis, i - 1], peer(axis, i))
+        return remote(idbuf.at[axis, me[axis]], idbuf.at[axis, me[axis]], id_s.at[axis, i - 1], id_r.at[axis, i - 1], peer(axis, i))
 
     for n in range(3):
         weight_local(n).start()
     for axis in range(3):
-        idbuf[axis, me[axis]] = idt[...]
+        idbuf[axis, me[axis]] = jnp.full((16, TOK), -1, jnp.int32)
+        for bt in (0, 1):
+            idbuf[axis, me[axis], bt * 8:bt * 8 + 6, :] = ids_n[bt][...]
 
     pl.semaphore_wait(barrier, 10)
     for axis in range(3):
         for i in (2, 1, 3):
             id_copy(axis, i).start()
-    for k in range(NCH):
-        start3(copy_d1, 0, k)
-    for n in range(3):
-        weight_remote(n).start()
 
     def iota(shape, dim):
         return lax.broadcasted_iota(jnp.int32, shape, dim)
 
     def build_comb(bt):
         ids, gates = ids_n[bt][...], gates_n[bt][...]
-        expert = iota((TOK, 64), 1)
-        hit = jnp.zeros((TOK, 64), f32)
-        gate = jnp.zeros((TOK, 64), f32)
-        for j in range(ids.shape[1]):
-            same = ids[:, j:j + 1] == expert
+        expert = iota((64, TOK), 0)
+        hit = jnp.zeros((64, TOK), f32)
+        gate = jnp.zeros((64, TOK), f32)
+        for j in range(6):
+            same = ids[j:j + 1, :] == expert
             hit = jnp.where(same, 1.0, hit)
-            gate = jnp.where(same, gates[:, j:j + 1], gate)
-        before = jnp.where(iota((TOK, TOK), 1) < iota((TOK, TOK), 0), 1.0, 0.0).astype(bf16)
-        count = jnp.dot(before, hit.astype(bf16), preferred_element_type=f32)
-        place = jnp.where((hit > 0.5) & (count < CAP - 0.5), count, -1.0)
+            gate = jnp.where(same, gates[j:j + 1, :], gate)
+        before = jnp.where(iota((TOK, TOK), 0) < iota((TOK, TOK), 1), 1.0, 0.0).astype(bf16)
+        count = jnp.dot(hit.astype(bf16), before, preferred_element_type=f32)
+        place = jnp.transpose(jnp.where((hit > 0.5) & (count < CAP - 0.5), count, -1.0))
+        gate = jnp.transpose(gate)
         spread = jnp.where(iota((64, 64 * SLOT), 1) // SLOT == iota((64, 64 * SLOT), 0), 1.0, 0.0).astype(bf16)
         wide = jnp.dot(place.astype(bf16), spread, preferred_element_type=f32)
         at_slot = wide == lax.rem(iota((TOK, 64 * SLOT), 1), SLOT).astype(f32)
@@ -226,29 +252,36 @@
             recv3(copy_d3, bt, k)
             local_d3(bt, k).wait()
 
-    def ffn(bt, m):
-        x = rows[bt, m].reshape(256, DIM)
-        total = None
-        for h in (0, 1):
-            g = jnp.dot(x, wg[h], preferred_element_type=f32)
-            u = jnp.dot(x, wu[h], preferred_element_type=f32)
-            hid = (jax.nn.silu(g) * u).astype(bf16)
-            part = jnp.dot(hid, wd[h], preferred_element_type=f32)
-            total = part if total is None else total + part
-        rows[bt, m] = total.astype(bf16).reshape(4, 4, SLOT, DIM)
-
-    def step_r1(bt):
-        for k in range(NCH):
-            start3(copy_r1, bt, k)
-        for k in range(NCH):
-            o, c0, w = CHUNKS[k]
-            cs = slice(c0, c0 + w)
-            if o == 0:
-                turn[bt, :, :, me[0], :, cs] = rows[bt, me[0], :, :, :, cs]
-            elif o == 1:
-                turn[bt, :, :, me[1], :, cs] = rows[bt, :, me[1], :, :, cs]
-            else:
-                turn[bt, :, :, me[2], :, cs] = rows[bt, :, :, me[2], :, cs]
+    def expert_step(step):
+        bt, part = step // 12, lax.rem(step, 3)
+        m = lax.rem(step, 12) // 3
+
+        @pl.when(part < 2)
+        def _():
+            x = rows[bt, m].reshape(256, DIM)
+            g = lax.dot_general(x, wg[part], (((1,), (1,)), ((), ())), preferred_element_type=f32)
+            u = lax.dot_general(x, wu[part], (((1,), (1,)), ((), ())), preferred_element_type=f32)
+            hid[part] = (jax.nn.silu(g) * u).astype(bf16)
+
+        @pl.when(part == 2)
+        def _():
+            total = jnp.dot(hid[0], wd[0], preferred_element_type=f32)
+            total = total + jnp.dot(hid[1], wd[1], preferred_element_type=f32)
+            rows[bt, m] = total.astype(bf16).reshape(4, 4, SLOT, DIM)
+
+    def step_d1(bt, k):
+        start3(copy_d1, bt, k)
+
+    def step_r1(bt, k):
+        start3(copy_r1, bt, k)
+        o, c0, w = CHUNKS[k]
+        cs = slice(c0, c0 + w)
+        if o == 0:
+            turn[bt, :, :, me[0], :, cs] = rows[bt, me[0], :, :, :, cs]
+        elif o == 1:
+            turn[bt, :, :, me[1], :, cs] = rows[bt, :, me[1], :, :, cs]
+        else:
+            turn[bt, :, :, me[2], :, cs] = rows[bt, :, :, me[2], :, cs]
 
     def step_r2(bt, k):
         recv3(copy_r1, bt, k)
@@ -267,59 +300,41 @@
         local_r3(bt, k).wait()
         vals = fin[bt, :, :, :, :, c0:c0 + w].reshape(64 * SLOT, w)
         got = jnp.dot(comb[bt], vals, preferred_element_type=f32)
-        outs[bt][:, c0:c0 + w] = (got[:TOK] + got[TOK:2 * TOK] + got[2 * TOK:]).astype(bf16)
-
-    for axis in range(3):
-        for i in (1, 3, 2):
-            id_copy(axis, i).wait_recv()
-    build_sel(0)
-    step_d2(0, 0)
-    step_d2(0, 1)
-    step_d2(0, 2)
-    for k in range(NCH):
-        start3(copy_d1, 1, k)
-    for k in range(3):
-        step_d2(0, k + 3)
-        step_d3(0, k)
-    build_sel(1)
-    for k in range(3):
-        step_d3(0, k + 3)
-        step_d2(1, k)
+        out[bt, :, c0:c0 + w] = (got[:TOK] + got[TOK:2 * TOK] + got[2 * TOK:]).astype(bf16)
+
+    todo = {"D1": step_d1, "D2": step_d2, "D3": step_d3, "R1": step_r1, "R2": step_r2, "R3": step_r3, "C": step_out,
+            "S": lambda bt, k: build_sel(bt), "W": lambda bt, k: build_comb(bt)}
+
+    def run(steps):
+        for name, bt, k in steps:
+            if (name, bt) == ("S", 0):
+                for n in range(3):
+                    weight_remote(n).start()
+                for axis in range(3):
+                    for i in (1, 3, 2):
+                        id_copy(axis, i).wait_recv()
+            todo[name](bt, k)
+
+    run(BEFORE)
     for n in range(3):
         weight_local(n).wait()
         weight_remote(n).wait_recv()
     wait_rows(0)
 
-    after = {
-        0: [lambda: step_d2(1, 3), lambda: step_d2(1, 4), lambda: step_d2(1, 5), lambda: step_d3(1, 0)],
-        1: [lambda: step_d3(1, 1), lambda: step_d3(1, 2), lambda: step_d3(1, 3)],
-        2: [lambda: step_d3(1, 4), lambda: step_d3(1, 5), lambda: build_comb(0), lambda: build_comb(1)],
-        3: [lambda: step_r1(0), lambda: wait_rows(1)],
-        4: [lambda: step_r2(0, 0), lambda: step_r2(0, 1), lambda: step_r2(0, 2)],
-        5: [lambda: step_r2(0, 3), lambda: step_r2(0, 4), lambda: step_r2(0, 5), lambda: step_r3(0, 0)],
-        6: [lambda: step_r3(0, 1), lambda: step_r3(0, 2), lambda: step_r3(0, 3)],
-        7: [lambda: step_r1(1), lambda: step_r3(0, 4), lambda: step_r3(0, 5)],
-    }
-
     def loop(step, carry):
-        ffn(step // 4, lax.rem(step, 4))
-        for at, todo in after.items():
+        @pl.when(step == 12)
+        def _():
+            wait_rows(1)
+
+        expert_step(step)
+        for at, steps in WHILE.items():
             @pl.when(step == at)
             def _():
-                for one in todo:
-                    one()
+                run(steps)
         return carry
 
-    lax.fori_loop(0, 8, loop, 0)
-
-    for k in range(NCH):
-        step_r2(1, k)
-        step_out(0, k)
-        if k >= 1:
-            step_r3(1, k - 1)
-    step_r3(1, NCH - 1)
-    for k in range(NCH):
-        step_out(1, k)
+    lax.fori_loop(0, 24, loop, 0)
+    run(AFTER)
 
     for axis in range(3):
         for i in (1, 2, 3):
@@ -345,20 +360,18 @@
     dma = pltpu.SemaphoreType.DMA
 
     def body(tok_a, ids_a, gate_a, tok_b, ids_b, gate_b, wg, wu, wd):
-        pad = ((0, 2), (0, 0))
-        idt = jnp.concatenate([jnp.pad(ids_a.T, pad, constant_values=-1), jnp.pad(ids_b.T, pad, constant_values=-1)])
         vmem = pl.BlockSpec(memory_space=pltpu.VMEM)
         hbm = pl.BlockSpec(memory_space=pl.ANY)
-        half = wg.shape[2]
+        half = wd.shape[1]
         box = (2, 4, 4, 4, SLOT, DIM)
         out = jax.ShapeDtypeStruct((TOK, DIM), bf16)
         relay = jax.ShapeDtypeStruct(box, bf16)
         stage = [dma((2, NCH, 3))] * 12
         res = pl.pallas_call(
             moe_kernel,
-            out_shape=(out, out, relay, relay),
-            in_specs=[hbm, hbm, vmem, vmem, vmem, vmem, vmem, hbm, hbm, hbm],
-            out_specs=(vmem, vmem, hbm, hbm),
+            out_shape=(jax.ShapeDtypeStruct((2, TOK, DIM), bf16), relay, relay),
+            in_specs=[hbm, hbm, vmem, vmem, vmem, vmem, hbm, hbm, hbm],
+            out_specs=(vmem, hbm, hbm),
             scratch_shapes=[
                 pltpu.VMEM((3, 4, 16, TOK), jnp.int32),
                 pltpu.VMEM((2, 4, TOK, DIM), bf16),
@@ -366,9 +379,10 @@
                 pltpu.VMEM(box, bf16),
                 pltpu.VMEM(box, bf16),
                 pltpu.VMEM(box, bf16),
-                pltpu.VMEM((2, DIM, half), bf16),
-                pltpu.VMEM((2, DIM, half), bf16),
                 pltpu.VMEM((2, half, DIM), bf16),
+                pltpu.VMEM((2, half, DIM), bf16),
+                pltpu.VMEM((2, half, DIM), bf16),
+                pltpu.VMEM((2, 256, half), bf16),
                 pltpu.VMEM((2, 3, 4, 256, TOK), bf16),
                 pltpu.VMEM((2, 3 * TOK, 64 * SLOT), bf16),
                 dma((3, 3)), dma((3, 3)), dma((3,)), dma((3,)), dma((3,)), dma((2, NCH)),
@@ -377,8 +391,8 @@
             ],
             compiler_params=pltpu.CompilerParams(collective_id=0, has_side_effects=True, vmem_limit_bytes=67043328),
             name="moe",
-        )(tok_a, tok_b, idt, ids_a, ids_b, gate_a, gate_b, wg, wu, wd)
-        return res[0], res[1]
+        )(tok_a, tok_b, ids_a.T, ids_b.T, gate_a.T, gate_b.T, wg.transpose(0, 2, 1), wu.transpose(0, 2, 1), wd)
+        return res[0][0], res[0][1]
 
     specs = (row_spec,) * 6 + (gate_spec, gate_spec, down_spec)
     return jax.shard_map(body, mesh=mesh, in_specs=specs, out_specs=(row_spec, row_spec), check_vma=False)

time: 219 us -> 187 us (0.85)
  Pallas kernels: 199 us -> 181 us
  local copies, waits for them, and re-layouts: 17 us -> 2.28 us
    pallas_call x1, Pallas kernels: 199 us -> 181 us  [body(): pl.pallas_call(moe_kernel, out_shape=(jax.ShapeDtypeStruct((2, TOK, DIM),...]
    unnamed x10 -> x0, local copies, waits for them, and re-layouts: 17 us -> none
    squeeze x0 -> x1, local copies, waits for them, and re-layouts: none -> 2.28 us  [body(): return (res[0][0], res[0][1])]
where the time goes in v2:
time: 187 us; the launch traced here: 184 us
  Pallas kernels  181 us (97%)
  local copies, waits for them, and re-layouts  2.28 us (1%)
    pallas_call x1, Pallas kernels, body(): pl.pallas_call(moe_kernel, out_shape=(jax.ShapeDtypeStruct((2, TOK, DIM),...  181 us

profile of v2, /device:TPU:3, one launch (start us, length us, event | category | flops | bytes accessed | tf_op | source)
XLA Modules:
  0.0 184.3 jit_solution(10815370656795232119)
XLA Ops:
  0.6 181.4 %moe.1 = (bf16[2,128,2048]{2,1,0:T(8,128)(2,1)}, bf16[2,4,4,4,16,2048]{5,4,3,2,1,0:T(8,128)(2,1)}, bf16[2,4,4,4,16,2048]{5,4,3,2,1,0:T(8,128)(2,1)}) custom-call(bf16[128,2048]{1,0:T(8,128)(2,1)} %tok_a.1, bf16[128,2048]{1,0:T(8,128)(2,1)} %tok_b.1, s32[6,128]{1,0:T(8,128)} %bitcast.12, s32[6,128]{1,0:T(8,128)} %bitcast.13, f32[6,128]{1,0:T(8,128)} %bitcast.14, ...), custom_call_target="tpu_custom_call" | custom-call | tf_op jit(solution)/shard_map/moe/pallas_call | solution.py:370
  182.0 2.3 %slice_bitcast_fusion = (bf16[128,2048]{1,0:T(8,128)(2,1)}, bf16[128,2048]{1,0:T(8,128)(2,1)}) fusion(bf16[2,128,2048]{2,1,0:T(8,128)(2,1)} %get-tuple-element.3), kind=kLoop, calls=%fused_computation | loop fusion | bytes 2097152 | tf_op jit(solution)/shard_map/squeeze | solution.py:395

commit v3 on v2

v3 whole, which is shorter than its diff:
```python
import jax
import jax.numpy as jnp
from jax import lax
from jax.experimental import pallas as pl
from jax.experimental.pallas import tpu as pltpu
from jax.sharding import PartitionSpec as P

MESH_ID = pl.DeviceIdType.MESH
SLOT = 16
CAP = 15
TOK = 128
DIM = 2048
MAIN = 1920
LANE = 128
STRIDE = (16, 4, 1)
FINE = ((0, 0, 384), (1, 384, 384), (2, 768, 384), (0, 1152, 256), (1, 1408, 256), (2, 1664, 256))
COARSE = ((0, 0, 640), (1, 640, 640), (2, 1280, 640))
IN, OUT = (FINE, FINE), (FINE, FINE)
NCH = len(FINE)
BEFORE = (
    "D1a5", "D1a1", "D1a0", "D1a2", "D1a3", "D1b1", "Wa0", "D1a4", "D1b0", "D1b3", "D1b2", "Sa0",
    "D2a1", "D1b4", "D2a3", "D2a5", "D2a0", "D1b5", "D2a4", "D2a2", "D3a5", "D3a3", "Sb0", "D3a1",
    "D3a4", "D3a0", "D3a2", "D2b1", "Wb0", "D2b0", "D2b3", "D2b5", "D2b2", "D2b4",
)
WHILE = {
    3: ("D3b1", "D3b5", "D3b0",),
    5: ("D3b2", "D3b4", "D3b3", "R1a0",),
    11: ("R1a1",),
    15: ("R2a2", "R2a1", "R2a0",),
    18: ("R2a5", "R1b0",),
    20: ("R2a3",),
    21: ("R2a4",),
    22: ("R3a2",),
}
AFTER = (
    "R1b1", "R3a4", "R3a0", "R2b2", "R2b0", "R2b5", "R3a5", "R2b3", "R3a3", "R2b1", "R3a1", "R2b4",
    "Ca3", "R3b0", "R3b1", "R3b2", "R3b3", "Ca5", "R3b4", "Ca0", "Ca1", "R3b5", "Ca2", "Cb1",
    "Ca4", "Cb0", "Cb2", "Cb4", "Cb3", "Cb5",
)


def moe_kernel(tok_a, tok_b, ids_a, ids_b, gate_a, gate_b, wg_in, wu_in, wd_in,
               out, relay_in, relay_out,
               idbuf, gath, gath_x, pairs, last, lift, x_last, out_last, comb_x, send2, rows, turn, fin, wg, wu, wd, hid, sel, comb,
               id_s, id_r, w_s, w_r, w_l, x_s, x_r,
               d1s, d1r, d2s, d2r, d3s, d3r, r1s, r1r, r2s, r2r, r3s, r3r):
    f32, bf16 = jnp.float32, jnp.bfloat16
    ep = lax.axis_index("ep")
    tp = lax.axis_index("tp")
    me = (ep // 16, lax.rem(ep // 4, 4), lax.rem(ep, 4))
    toks = (tok_a, tok_b)
    ids_n, gates_n = (ids_a, ids_b), (gate_a, gate_b)

    def shifted(axis, step):
        return lax.rem(me[axis] + step, 4)

    def peer(axis, step):
        return {"ep": ep + (shifted(axis, step) - me[axis]) * STRIDE[axis]}

    def remote(src, dst, s_sem, r_sem, dev):
        return pltpu.make_async_remote_copy(src, dst, s_sem, r_sem, device_id=dev, device_id_type=MESH_ID)

    def cols(chunk):
        return pl.ds(chunk[1], chunk[2])

    def fixed_canon(buf, bt, axis, at, chunk):
        if axis == 0:
            return buf.at[bt, at, :, :, :, cols(chunk)]
        if axis == 1:
            return buf.at[bt, :, at, :, :, cols(chunk)]
        return buf.at[bt, :, :, at, :, cols(chunk)]

    def relay_slot(buf, bt, o, chunk, at):
        if o == 2:
            return buf.at[bt, :, at, :, :, cols(chunk)]
        return buf.at[bt, :, :, at, :, cols(chunk)]

    def copy_d1(bt, k, i):
        o = IN[bt][k][0]
        return remote(toks[bt].at[:, cols(IN[bt][k])], gath.at[bt, me[o], :, cols(IN[bt][k])],
                      d1s.at[bt], d1r.at[bt, k], peer(o, i))

    def local_d1(bt, k):
        o = IN[bt][k][0]
        return pltpu.make_async_copy(toks[bt].at[:, cols(IN[bt][k])], gath.at[bt, me[o], :, cols(IN[bt][k])], d1r.at[bt, k])

    def copy_x(bt, o, i):
        return remote(toks[bt].at[:, pl.ds(MAIN, LANE)], gath_x.at[bt, o, me[o]],
                      x_s.at[bt], x_r.at[bt, o], peer(o, i))

    def local_x(bt, o):
        return pltpu.make_async_copy(toks[bt].at[:, pl.ds(MAIN, LANE)], gath_x.at[bt, o, me[o]], x_r.at[bt, o])

    def copy_d2(bt, k, i):
        o = IN[bt][k][0]
        b = (o + 1) % 3
        return remote(send2.at[shifted(b, i), :, :, :, cols(IN[bt][k])], relay_slot(relay_in, bt, o, IN[bt][k], me[b]),
                      d2s.at[bt], d2r.at[bt, k], peer(b, i))

    def local_d2(bt, k):
        o = IN[bt][k][0]
        b = (o + 1) % 3
        return pltpu.make_async_copy(send2.at[me[b], :, :, :, cols(IN[bt][k])], relay_slot(relay_in, bt, o, IN[bt][k], me[b]), d2r.at[bt, k])

    def copy_3(src, dst, s, r, chunk, bt, k, i):
        c = (chunk[0] + 2) % 3
        return remote(src.at[bt, shifted(c, i), :, :, :, cols(chunk)], fixed_canon(dst, bt, c, me[c], chunk),
                      s.at[bt], r.at[bt, k], peer(c, i))

    def local_3(src, dst, sem, chunk, bt, k):
        c = (chunk[0] + 2) % 3
        return pltpu.make_async_copy(src.at[bt, me[c], :, :, :, cols(chunk)], fixed_canon(dst, bt, c, me[c], chunk), sem.at[bt, k])

    far = 2 * (1 - me[0] // 2)

    def copy_r1(bt, k, i, h):
        o = OUT[bt][k][0]
        cs = cols(OUT[bt][k])
        planes = pl.ds(lax.rem(far + 2 * h, 4), 2)
        if o == 0:
            src, dst = rows.at[bt, shifted(0, i), :, :, :, cs], turn.at[bt, :, :, me[0], :, cs]
        elif o == 1:
            src, dst = rows.at[bt, planes, shifted(1, i), :, :, cs], turn.at[bt, planes, :, me[1], :, cs]
        else:
            src, dst = rows.at[bt, planes, :, shifted(2, i), :, cs], turn.at[bt, planes, :, me[2], :, cs]
        return remote(src, dst, r1s.at[bt], r1r.at[bt, k], peer(o, i))

    def turn_part(bt, k, at):
        if OUT[bt][k][0] == 1:
            return turn.at[bt, :, at, :, :, cols(OUT[bt][k])]
        return turn.at[bt, at, :, :, :, cols(OUT[bt][k])]

    def copy_r2(bt, k, i):
        o = OUT[bt][k][0]
        b = (o + 1) % 3
        return remote(turn_part(bt, k, shifted(b, i)), relay_slot(relay_out, bt, o, OUT[bt][k], me[b]),
                      r2s.at[bt], r2r.at[bt, k], peer(b, i))

    def local_r2(bt, k):
        o = OUT[bt][k][0]
        b = (o + 1) % 3
        return pltpu.make_async_copy(turn_part(bt, k, me[b]), relay_slot(relay_out, bt, o, OUT[bt][k], me[b]), r2r.at[bt, k])

    def copy_d3(bt, k, i):
        return copy_3(relay_in, rows, d3s, d3r, IN[bt][k], bt, k, i)

    def copy_r3(bt, k, i):
        return copy_3(relay_out, fin, r3s, r3r, OUT[bt][k], bt, k, i)

    def local_d3(bt, k):
        return local_3(relay_in, rows, d3r, IN[bt][k], bt, k)

    def local_r3(bt, k):
        return local_3(relay_out, fin, r3r, OUT[bt][k], bt, k)

    def start3(copy, bt, k):
        for i in (2, 1, 3):
            copy(bt, k, i).start()

    def drain(ref, sem):
        pltpu.make_async_copy(ref, ref, sem).wait()

    def arrived(buf, sem, bt, k, chunk):
        drain(buf.at[bt, :, :, :, :, cols(chunk)], sem.at[bt, k])

    def iota(shape, dim):
        return lax.broadcasted_iota(jnp.int32, shape, dim)

    def build_moves():
        row, col = iota((256, 256), 0), iota((256, 256), 1)
        pairs[...] = jnp.where(((row >> 4) == (col & 15)) & ((row & 15) == (col >> 4)), 1.0, 0.0).astype(bf16)
        last[...] = jnp.where(iota((128, 1024), 1) == iota((128, 1024), 0) * SLOT + CAP, 1.0, 0.0).astype(bf16)
        lift[...] = jnp.where(iota((256, SLOT), 0) == iota((256, SLOT), 1) * SLOT + CAP, 1.0, 0.0).astype(bf16)

    def fold(block, first, count):
        swapped = jnp.dot(pairs[...], block, preferred_element_type=f32).astype(bf16)
        parts = [swapped[j * SLOT:(j + 1) * SLOT] for j in range(first, first + count)]
        return jnp.concatenate(parts, axis=1)

    def build_comb(bt):
        ids, gates = ids_n[bt][...], gates_n[bt][...]
        expert = iota((64, TOK), 0)
        hit = jnp.zeros((64, TOK), f32)
        gate = jnp.zeros((64, TOK), f32)
        for j in range(6):
            same = ids[j:j + 1, :] == expert
            hit = jnp.where(same, 1.0, hit)
            gate = jnp.where(same, gates[j:j + 1, :], gate)
        before = jnp.where(iota((TOK, TOK), 0) < iota((TOK, TOK), 1), 1.0, 0.0).astype(bf16)
        count = jnp.dot(hit.astype(bf16), before, preferred_element_type=f32)
        place = jnp.transpose(jnp.where((hit > 0.5) & (count < CAP - 0.5), count, -1.0))
        gate = jnp.transpose(gate)
        spread = jnp.where((iota((64, 64 * SLOT), 1) >> 4) == iota((64, 64 * SLOT), 0), 1.0, 0.0).astype(bf16)
        wide = jnp.dot(place.astype(bf16), spread, preferred_element_type=f32)
        at_slot = wide == (iota((TOK, 64 * SLOT), 1) & 15).astype(f32)
        spread_x = jnp.where((iota((64, MAIN), 1) & 127) == iota((64, MAIN), 0), 1.0, 0.0).astype(bf16)
        wide_x = jnp.dot(place.astype(bf16), spread_x, preferred_element_type=f32)
        at_slot_x = wide_x == (iota((TOK, MAIN), 1) >> 7).astype(f32)
        rest = gate
        for n in range(3):
            part = rest.astype(bf16)
            rest = rest - part.astype(f32)
            part_wide = jnp.dot(part, spread, preferred_element_type=f32)
            comb[bt, n * TOK:(n + 1) * TOK, :] = jnp.where(at_slot, part_wide, 0.0).astype(bf16)
            part_wide = jnp.dot(part, spread_x, preferred_element_type=f32)
            comb_x[bt, n * TOK:(n + 1) * TOK, :] = jnp.where(at_slot_x, part_wide, 0.0).astype(bf16)

    def build_sel(bt):
        before = jnp.where(iota((TOK, TOK), 0) < iota((TOK, TOK), 1), 1.0, 0.0).astype(bf16)
        for o in range(3):
            b, c = (o + 1) % 3, (o + 2) % 3
            row = iota((16, TOK), 0)
            expert = me[o] * STRIDE[o] + (row >> 2) * STRIDE[b] + (row & 3) * STRIDE[c]
            for a in range(4):
                ids = idbuf[o, a, bt * 8:bt * 8 + 8, :]
                hit = jnp.zeros((16, TOK), f32)
                for j in range(6):
                    hit = jnp.where(ids[j:j + 1, :] == expert, 1.0, hit)
                count = jnp.dot(hit.astype(bf16), before, preferred_element_type=f32)
                place = jnp.where((hit > 0.5) & (count < CAP - 0.5), count, -1.0)
                slot = iota((SLOT, TOK), 0).astype(f32)
                for r in range(16):
                    sel[bt, o, a, r * SLOT:(r + 1) * SLOT, :] = jnp.where(place[r:r + 1, :] == slot, 1.0, 0.0).astype(bf16)

    barrier = pltpu.get_barrier_semaphore()
    for axis in range(3):
        for i in (1, 2, 3):
            pl.semaphore_signal(barrier, inc=1, device_id=peer(axis, i), device_id_type=MESH_ID)
    other = {"tp": 1 - tp}
    pl.semaphore_signal(barrier, inc=1, device_id=other, device_id_type=MESH_ID)
    for bt in (0, 1):
        for k in range(len(IN[bt])):
            local_d1(bt, k).start()
        for o in range(3):
            local_x(bt, o).start()
    weights = ((wg_in, wg), (wu_in, wu), (wd_in, wd))

    def weight_local(n):
        src, dst = weights[n]
        return pltpu.make_async_copy(src.at[0], dst.at[tp], w_l.at[n])

    def weight_remote(n):
        src, dst = weights[n]
        return remote(src.at[0], dst.at[tp], w_s.at[n], w_r.at[n], other)

    def id_copy(axis, i):
        return remote(idbuf.at[axis, me[axis]], idbuf.at[axis, me[axis]], id_s.at[0], id_r.at[0], peer(axis, i))

    for axis in range(3):
        idbuf[axis, me[axis]] = jnp.full((16, TOK), -1, jnp.int32)
        for bt in (0, 1):
            idbuf[axis, me[axis], bt * 8:bt * 8 + 6, :] = ids_n[bt][...]

    pl.semaphore_wait(barrier, 10)
    for axis in range(3):
        for i in (2, 1, 3):
            id_copy(axis, i).start()

    seen_x, sent_x, reused, left = set(), set(), [], [0, 0]

    def step_d2(bt, k):
        o, c0, w = IN[bt][k]
        drain(gath.at[bt, :, :, cols(IN[bt][k])], d1r.at[bt, k])
        if bt == 1 and not reused:
            reused.append(True)
            drain(send2.at[pl.ds(0, 3)], d2s.at[0])
        if (bt, o) not in seen_x:
            seen_x.add((bt, o))
            drain(gath_x.at[bt, o], x_r.at[bt, o])
        for a in range(4):
            tail = jnp.dot(sel[bt, o, a], gath_x[bt, o, a], preferred_element_type=f32).astype(bf16)
            got = jnp.dot(sel[bt, o, a], gath[bt, a, :, c0:c0 + w], preferred_element_type=f32)
            got = got + jnp.dot(lift[...], fold(tail, c0 // LANE, w // LANE), preferred_element_type=f32)
            send2[:, :, a, :, c0:c0 + w] = got.astype(bf16).reshape(4, 4, SLOT, w)
        start3(copy_d2, bt, k)
        local_d2(bt, k).start()

    def step_d3(bt, k):
        arrived(relay_in, d2r, bt, k, IN[bt][k])
        start3(copy_d3, bt, k)
        local_d3(bt, k).start()

    def wait_rows(bt):
        for k in range(len(IN[bt])):
            arrived(rows, d3r, bt, k, IN[bt][k])

    def expert_step(step):
        bt, part = step // 12, lax.rem(step, 3)
        m = lax.rem(far + lax.rem(step, 12) // 3, 4)

        @pl.when(part < 2)
        def _():
            x = rows[bt, m].reshape(256, MAIN)

            @pl.when(part == 0)
            def _():
                ends = jnp.dot(last[:SLOT, :256], x, preferred_element_type=f32).astype(bf16)
                tiles = [ends[:, j * LANE:(j + 1) * LANE] for j in range(CAP)] + [jnp.zeros((SLOT, LANE), bf16)]
                x_last[...] = jnp.dot(pairs[...], jnp.concatenate(tiles, axis=0), preferred_element_type=f32).astype(bf16)

            x = jnp.concatenate([x, x_last[...]], axis=1)
            g = lax.dot_general(x, wg[part], (((1,), (1,)), ((), ())), preferred_element_type=f32)
            u = lax.dot_general(x, wu[part], (((1,), (1,)), ((), ())), preferred_element_type=f32)
            hid[part] = (jax.nn.silu(g) * u).astype(bf16)

        @pl.when(part == 2)
        def _():
            total = jnp.dot(hid[0], wd[0], preferred_element_type=f32)
            total = total + jnp.dot(hid[1], wd[1], preferred_element_type=f32)
            folded = fold(total[:, MAIN:].astype(bf16), 0, CAP)
            lifted = jnp.dot(lift[...], folded, preferred_element_type=f32)
            kept = jnp.where((iota((256, MAIN), 0) & 15) == CAP, lifted, total[:, :MAIN])
            rows[bt, m] = kept.astype(bf16).reshape(4, 4, SLOT, MAIN)

    def step_d1(bt, k):
        o = IN[bt][k][0]
        if (bt, o) not in sent_x:
            sent_x.add((bt, o))
            start3(copy_x, bt, o)
        start3(copy_d1, bt, k)

    def step_r1(bt, h):
        for k in range(len(OUT[bt])):
            if OUT[bt][k][0] == 0:
                near = me[0] + 1 - 2 * lax.rem(me[0], 2)
                for z in (far, far + 1) if h == 0 else (near,):
                    copy_r1(bt, k, lax.rem(z - me[0] + 4, 4), 0).start()
            else:
                for i in (2, 1, 3):
                    copy_r1(bt, k, i, h).start()
        planes = pl.ds(lax.rem(far + 2 * h, 4), 2)
        for o, c0, w in OUT[bt]:
            cs = slice(c0, c0 + w)
            if o == 0 and h == 1:
                turn[bt, :, :, me[0], :, cs] = rows[bt, me[0], :, :, :, cs]
            elif o == 1:
                turn[bt, planes, :, me[1], :, cs] = rows[bt, planes, me[1], :, :, cs]
            elif o == 2:
                turn[bt, planes, :, me[2], :, cs] = rows[bt, planes, :, me[2], :, cs]

    def step_r2(bt, k):
        drain(turn.at[bt, pl.ds(0, 3), :, :, :, cols(OUT[bt][k])], r1r.at[bt, k])
        start3(copy_r2, bt, k)
        local_r2(bt, k).start()

    def step_r3(bt, k):
        arrived(relay_out, r2r, bt, k, OUT[bt][k])
        start3(copy_r3, bt, k)
        local_r3(bt, k).start()

    def step_out(bt, k):
        o, c0, w = OUT[bt][k]
        arrived(fin, r3r, bt, k, OUT[bt][k])
        vals = fin[bt, :, :, :, :, c0:c0 + w].reshape(64 * SLOT, w)
        got = jnp.dot(comb[bt], vals, preferred_element_type=f32)
        out[bt, :, c0:c0 + w] = (got[:TOK] + got[TOK:2 * TOK] + got[2 * TOK:]).astype(bf16)
        ends = jnp.dot(last[...], vals, preferred_element_type=f32).astype(bf16)
        tiles = jnp.concatenate([ends[:, j * LANE:(j + 1) * LANE] for j in range(w // LANE)], axis=0)
        got = jnp.dot(comb_x[bt, :, c0:c0 + w], tiles, preferred_element_type=f32)
        total = got[:TOK] + got[TOK:2 * TOK] + got[2 * TOK:]
        if left[bt]:
            total = out_last[bt] + total
        left[bt] += 1
        if left[bt] < len(OUT[bt]):
            out_last[bt] = total
        else:
            out[bt, :, MAIN:] = total.astype(bf16)

    todo = {"D1": step_d1, "D2": step_d2, "D3": step_d3, "R1": step_r1, "R2": step_r2, "R3": step_r3, "C": step_out,
            "S": lambda bt, k: build_sel(bt), "W": lambda bt, k: build_comb(bt)}

    def run(steps):
        for step in steps:
            name, bt, k = step[:-2], "ab".index(step[-2]), int(step[-1])
            if (name, bt) == ("S", 0):
                for n in range(3):
                    weight_local(n).start()
                    weight_remote(n).start()
                build_moves()
                drain(idbuf.at[:, pl.ds(0, 3)], id_r.at[0])
            todo[name](bt, k)

    run(BEFORE)
    for n in range(3):
        weight_local(n).wait()
        weight_remote(n).wait_recv()
    wait_rows(0)

    def loop(step, carry):
        @pl.when(step == 12)
        def _():
            wait_rows(1)

        expert_step(step)
        for at, steps in WHILE.items():
            @pl.when(step == at)
            def _():
                run(steps)
        return carry

    lax.fori_loop(0, 24, loop, 0)
    run(AFTER)

    drain(idbuf.at[:, pl.ds(0, 3)], id_s.at[0])
    for n in range(3):
        weight_remote(n).wait_send()
    drain(send2.at[pl.ds(0, 3)], d2s.at[1])
    for bt in (0, 1):
        drain(gath.at[bt, pl.ds(0, 3)], d1s.at[bt])
        drain(gath_x.at[bt, :, pl.ds(0, 3)], x_s.at[bt])
        drain(rows.at[bt, pl.ds(0, 3)], d3s.at[bt])
        drain(rows.at[bt, pl.ds(0, 3)], r1s.at[bt])
        drain(turn.at[bt, pl.ds(0, 3)], r2s.at[bt])
        drain(fin.at[bt, pl.ds(0, 3)], r3s.at[bt])


def solution(mesh):
    row_spec = P(("dp", "ep", "tp"), None)
    gate_spec = P("ep", None, "tp")
    down_spec = P("ep", "tp", None)
    bf16 = jnp.bfloat16
    dma = pltpu.SemaphoreType.DMA

    def body(tok_a, ids_a, gate_a, tok_b, ids_b, gate_b, wg, wu, wd):
        vmem = pl.BlockSpec(memory_space=pltpu.VMEM)
        hbm = pl.BlockSpec(memory_space=pl.ANY)
        half = wd.shape[1]
        box = (2, 4, 4, 4, SLOT, MAIN)
        out = jax.ShapeDtypeStruct((TOK, DIM), bf16)
        relay = jax.ShapeDtypeStruct(box, bf16)
        res = pl.pallas_call(
            moe_kernel,
            out_shape=(jax.ShapeDtypeStruct((2, TOK, DIM), bf16), relay, relay),
            in_specs=[hbm, hbm, vmem, vmem, vmem, vmem, hbm, hbm, hbm],
            out_specs=(vmem, hbm, hbm),
            scratch_shapes=[
                pltpu.VMEM((3, 4, 16, TOK), jnp.int32),
                pltpu.VMEM((2, 4, TOK, MAIN), bf16),
                pltpu.VMEM((2, 3, 4, TOK, LANE), bf16),
                pltpu.VMEM((256, 256), bf16),
                pltpu.VMEM((128, 1024), bf16),
                pltpu.VMEM((256, SLOT), bf16),
                pltpu.VMEM((256, LANE), bf16),
                pltpu.VMEM((2, TOK, LANE), jnp.float32),
                pltpu.VMEM((2, 3 * TOK, MAIN), bf16),
                pltpu.VMEM((4, 4, 4, SLOT, MAIN), bf16),
                pltpu.VMEM(box, bf16),
                pltpu.VMEM(box, bf16),
                pltpu.VMEM(box, bf16),
                pltpu.VMEM((2, half, DIM), bf16),
                pltpu.VMEM((2, half, DIM), bf16),
                pltpu.VMEM((2, half, DIM), bf16),
                pltpu.VMEM((2, 256, half), bf16),
                pltpu.VMEM((2, 3, 4, 256, TOK), bf16),
                pltpu.VMEM((2, 3 * TOK, 64 * SLOT), bf16),
                dma((1,)), dma((1,)), dma((3,)), dma((3,)), dma((3,)), dma((2,)), dma((2, 3)),
                *([dma((2,)), dma((2, NCH))] * 6),
            ],
            compiler_params=pltpu.CompilerParams(collective_id=0, has_side_effects=True, vmem_limit_bytes=67043328),
            name="moe",
        )(tok_a, tok_b, ids_a.T, ids_b.T, gate_a.T, gate_b.T, wg.transpose(0, 2, 1), wu.transpose(0, 2, 1), wd)
        return res[0][0], res[0][1]

    specs = (row_spec,) * 6 + (gate_spec, gate_spec, down_spec)
    return jax.shard_map(body, mesh=mesh, in_specs=specs, out_specs=(row_spec, row_spec), check_vma=False)
```

time: 187 us -> 175 us (0.936)
  the two profiles are of different devices: /device:TPU:3 before, /device:TPU:8 now
where the time goes in v3:
time: 175 us
  Pallas kernels  172 us (98%)
  local copies, waits for them, and re-layouts  2.28 us (1%)
    pallas_call x1, Pallas kernels, body(): pl.pallas_call(moe_kernel, out_shape=(jax.ShapeDtypeStruct((2, TOK, DIM),...  172 us

profile of v3, /device:TPU:8, one launch (start us, length us, event | category | flops | bytes accessed | tf_op | source)
XLA Modules:
  0.0 175.1 jit_solution(4153832353486898481)
XLA Ops:
  0.6 172.2 %moe.1 = (bf16[2,128,2048]{2,1,0:T(8,128)(2,1)}, bf16[2,4,4,4,16,1920]{5,4,3,2,1,0:T(8,128)(2,1)}, bf16[2,4,4,4,16,1920]{5,4,3,2,1,0:T(8,128)(2,1)}) custom-call(bf16[128,2048]{1,0:T(8,128)(2,1)} %tok_a.1, bf16[128,2048]{1,0:T(8,128)(2,1)} %tok_b.1, s32[6,128]{1,0:T(8,128)} %bitcast.12, s32[6,128]{1,0:T(8,128)} %bitcast.13, f32[6,128]{1,0:T(8,128)} %bitcast.14, ...), custom_call_target="tpu_custom_call" | custom-call | tf_op jit(solution)/shard_map/moe/pallas_call | solution.py:431
  172.8 2.3 %slice_bitcast_fusion = (bf16[128,2048]{1,0:T(8,128)(2,1)}, bf16[128,2048]{1,0:T(8,128)(2,1)}) fusion(bf16[2,128,2048]{2,1,0:T(8,128)(2,1)} %get-tuple-element.3), kind=kLoop, calls=%fused_computation | loop fusion | bytes 2097152 | tf_op jit(solution)/shard_map/squeeze | solution.py:462

commit v4 on v3

--- a/solution.py
+++ b/solution.py
@@ -154,7 +154,7 @@
         return local_3(relay_out, fin, r3r, OUT[bt][k], bt, k)
 
     def start3(copy, bt, k):
-        for i in (2, 1, 3):
+        for i in (1, 3, 2):
             copy(bt, k, i).start()
 
     def drain(ref, sem):
@@ -369,13 +369,17 @@
     todo = {"D1": step_d1, "D2": step_d2, "D3": step_d3, "R1": step_r1, "R2": step_r2, "R3": step_r3, "C": step_out,
             "S": lambda bt, k: build_sel(bt), "W": lambda bt, k: build_comb(bt)}
 
+    swapped = []
+
     def run(steps):
         for step in steps:
             name, bt, k = step[:-2], "ab".index(step[-2]), int(step[-1])
-            if (name, bt) == ("S", 0):
+            if (name, bt) == ("D3", 0) and not swapped:
+                swapped.append(True)
                 for n in range(3):
                     weight_local(n).start()
                     weight_remote(n).start()
+            if (name, bt) == ("S", 0):
                 build_moves()
                 drain(idbuf.at[:, pl.ds(0, 3)], id_r.at[0])
             todo[name](bt, k)

time: 175 us -> 175 us (level)
  the two profiles are of different devices: /device:TPU:8 before, /device:TPU:28 now
where the time goes in v4:
time: 175 us
  Pallas kernels  172 us (98%)
  local copies, waits for them, and re-layouts  2.28 us (1%)
    pallas_call x1, Pallas kernels, body(): pl.pallas_call(moe_kernel, out_shape=(jax.ShapeDtypeStruct((2, TOK, DIM),...  172 us

profile of v4, /device:TPU:28, one launch (start us, length us, event | category | flops | bytes accessed | tf_op | source)
XLA Modules:
  0.0 175.3 jit_solution(7800428601509739561)
XLA Ops:
  0.6 172.4 %moe.1 = (bf16[2,128,2048]{2,1,0:T(8,128)(2,1)}, bf16[2,4,4,4,16,1920]{5,4,3,2,1,0:T(8,128)(2,1)}, bf16[2,4,4,4,16,1920]{5,4,3,2,1,0:T(8,128)(2,1)}) custom-call(bf16[128,2048]{1,0:T(8,128)(2,1)} %tok_a.1, bf16[128,2048]{1,0:T(8,128)(2,1)} %tok_b.1, s32[6,128]{1,0:T(8,128)} %bitcast.12, s32[6,128]{1,0:T(8,128)} %bitcast.13, f32[6,128]{1,0:T(8,128)} %bitcast.14, ...), custom_call_target="tpu_custom_call" | custom-call | tf_op jit(solution)/shard_map/moe/pallas_call | solution.py:435
  173.0 2.3 %slice_bitcast_fusion = (bf16[128,2048]{1,0:T(8,128)(2,1)}, bf16[128,2048]{1,0:T(8,128)(2,1)}) fusion(bf16[2,128,2048]{2,1,0:T(8,128)(2,1)} %get-tuple-element.3), kind=kLoop, calls=%fused_computation | loop fusion | bytes 2097152 | tf_op jit(solution)/shard_map/squeeze | solution.py:466
